TPU v7x, 512 devices: a whole 4x8x8 slice. The times are simulated.
512 devices in a mesh: lon: 32 (over y_hi, z, core), lat: 16 (over y_lo, x).
Axes of the slice: x: 4, y: 8 (y_hi: 2, y_lo: 4; y = y_hi * 4 + y_lo), z: 8, core: 2. Of those that a mesh axis runs over, the one named last changes fastest.
Arguments:
- fine_input: bfloat16 [4, 192, 768, 384], P(None, 'lat', 'lon'), may hold values from -10 to 10
- merge_gain: float32 [1536], replicated, may hold values from 0.5 to 1.5
- merge_bias: float32 [1536], replicated, may hold values from -1.5 to 1.5
- merge_weight: bfloat16 [1536, 768], P('lat'), may hold values from -2 to 2
- coarse_gain: float32 [768], replicated, may hold values from 0.5 to 1.5
- coarse_bias: float32 [768], replicated, may hold values from -1.5 to 1.5
- coarse_qkv: bfloat16 [768, 2304], P('lat'), may hold values from -2 to 2
- coarse_out: bfloat16 [768, 768], P('lat'), may hold values from -0.21875 to 0.21875
Outputs:
- coarse_output: bfloat16 [4, 96, 384, 768], P(None, 'lat', 'lon')
All inputs are finite; a program needn't handle non-finite values.
Results may differ from a plain program's by a relative error of at most 0.013.
Values may be sent and summed in bfloat16 or wider, within the bound.
No kernel may reach another device: no remote copies, remote signals or barrier semaphores. Data moves between devices by JAX's collectives and lax.ppermute only.
A program may use at most 128 MiB of HBM per device.

v0:
```python
import jax
import jax.numpy as jnp
from jax import lax
from jax.experimental import pallas as pl
from jax.experimental.pallas import tpu as pltpu
from jax.sharding import PartitionSpec as P


EPSILON = 1e-05
AXES = ("lon", "lat")
F32 = jnp.float32
BF16 = jnp.bfloat16

DEVICES = 512


def coords_of(flat):
    lat, lon = flat % 16, flat // 16
    return lat % 4, (lon // 16) * 4 + lat // 4, lon // 2 % 8, lon % 2


def flat_of(x, y, z, core):
    x, y, z = x % 4, y % 8, z % 8
    return (((y // 4) * 8 + z) * 2 + core) * 16 + (y % 4) * 4 + x


def ring_step(dx, dy, x, y):
    if dy == 2:
        dy = 2 if y % 2 == 0 else -2
    return x + dx, y + dy


def far_pairs(step):
    pairs = []
    for flat in range(DEVICES):
        x, y, z, core = coords_of(flat)
        nx, ny = ring_step(step if core == 1 else 0, step if core == 0 else 0, x, y)
        pairs.append((flat, flat_of(nx, ny, z, core)))
    return pairs


def near_groups():
    groups = {}
    for flat in range(DEVICES):
        x, y, z, core = coords_of(flat)
        key = (core, y, z) if core == 0 else (core, x, z, y // 4)
        groups.setdefault(key, []).append((x if core == 0 else y, flat))
    return [[flat for _, flat in sorted(group)] for group in groups.values()]


def swap_pairs():
    pairs = []
    for flat in range(DEVICES):
        x, y, z, core = coords_of(flat)
        pairs.append((flat, flat_of(x, y, z, 1 - core)))
    return pairs


def shift_pairs(dlon, dlat, back=False):
    pairs = []
    for flat in range(DEVICES):
        lon, lat = flat // 16, flat % 16
        sign = 1 if lon % 2 == 0 else -1
        target = (lon + dlon) % 32 * 16 + (lat + sign * dlat) % 16
        pairs.append((target, flat) if back else (flat, target))
    return pairs


def moved(value, pairs):
    return lax.ppermute(value, AXES, pairs)


STEPS = (0, -1, 1, 2)


def dot(a, b):
    return jnp.dot(a, b, preferred_element_type=F32)


def normalize(values, gain, bias):
    average = jnp.mean(values, axis=-1, keepdims=True)
    centered = values - average
    spread = jnp.mean(centered * centered, axis=-1, keepdims=True)
    return centered * lax.rsqrt(spread + EPSILON) * gain + bias


def cut_kernel(fine_ref, merge_hbm, qkv_hbm, out_hbm, left_ref, held_hbm, sems):
    core = lax.axis_index("lon") % 2
    for side in range(2):

        @pl.when(core == side)
        def _():
            cuts = [(merge_hbm, side * 384, 0, 96), (out_hbm, side * 384, 240, 48)]
            cuts += [(qkv_hbm, side * 1152 + n * 384, 96 + n * 48, 48) for n in range(3)]
            copies = []
            for member in range(4):
                for n, (source, column, row, rows) in enumerate(cuts):
                    copies.append(
                        pltpu.make_async_copy(
                            source.at[:, pl.ds(column, 384)],
                            held_hbm.at[member, pl.ds(row, rows), :],
                            sems.at[member * 5 + n],
                        )
                    )
            for copy in copies:
                copy.start()
            row = lax.broadcasted_iota(jnp.int32, (144, 1), 0)
            source = lax.broadcasted_iota(jnp.int32, (144, 288), 1)
            pick = jnp.where(source == row // 12 * 24 + row % 12, 1.0, 0.0).astype(BF16)
            for level in range(4):
                part = dot(pick, fine_ref[level * 288 : level * 288 + 288])
                left_ref[level * 144 : level * 144 + 144] = part.astype(BF16)
            for copy in copies:
                copy.wait()


def cut(fine, weights):
    vmem = pl.BlockSpec(memory_space=pltpu.VMEM)
    return pl.pallas_call(
        cut_kernel,
        out_shape=(
            jax.ShapeDtypeStruct((576, 384), BF16),
            jax.ShapeDtypeStruct((4, 288, 384), BF16),
        ),
        in_specs=[vmem] * 4,
        out_specs=(vmem, vmem),
        scratch_shapes=[pltpu.SemaphoreType.DMA((20,))],
        name="cut",
        cost_estimate=pl.CostEstimate(flops=1_000_000, bytes_accessed=1_800_000, transcendentals=0),
    )(fine, *weights)


def patch_kernel(
    fine_hbm, left_hbm, gain_hbm, bias_hbm, near_ref, far_ref, fine_ref, left_ref, gain_ref, bias_ref, sems
):
    core = lax.axis_index("lon") % 2
    loads = [
        pltpu.make_async_copy(source, target, sems.at[n])
        for n, (source, target) in enumerate(
            ((fine_hbm, fine_ref), (left_hbm, left_ref), (gain_hbm, gain_ref), (bias_hbm, bias_ref))
        )
    ]
    for load in loads:
        load.start()
    row = lax.broadcasted_iota(jnp.int32, (72, 1), 0)
    level, a, b = row // 18, row % 18 // 6, row % 6
    own_at = level * 144 + a * 48 + (6 + b) * 2
    next_at = level * 144 + a * 24 + b * 2
    source = lax.broadcasted_iota(jnp.int32, (72, 576), 1)

    def picks(base, places):
        return [jnp.where(source == base + at, 1.0, 0.0).astype(BF16) for at in places]

    own_picks = picks(own_at, (0, 1, 24, 25))
    for load in loads:
        load.wait()
    for half, ref in ((1 - core, near_ref), (core, far_ref)):
        own = jnp.concatenate(
            [
                fine_ref[pl.ds(pl.multiple_of(level * 288 + half * 144, 144), 144), :]
                for level in range(4)
            ],
            axis=0,
        )
        next_picks = picks(next_at + half * 72, (0, 1, 12, 13))
        for first, fine, chosen in ((0, own, own_picks), (72, left_ref[...], next_picks)):
            parts = [dot(pick, fine) for pick in chosen]
            total = parts[0] + parts[1] + parts[2] + parts[3]
            average = jnp.sum(total, axis=-1, keepdims=True) / 1536
            parts = [part - average for part in parts]
            squares = sum(part * part for part in parts)
            scale = lax.rsqrt(jnp.sum(squares, axis=-1, keepdims=True) / 1536 + EPSILON)
            for k in range(4):
                cols = slice(k * 384, (k + 1) * 384)
                gain, bias = gain_ref[cols].reshape(1, 384), bias_ref[cols].reshape(1, 384)
                ref[first : first + 72, cols] = (parts[k] * scale * gain + bias).astype(BF16)


def patches(fine, left, gain, bias):
    pack = jax.ShapeDtypeStruct((144, 1536), BF16)
    operands = (fine, left, gain, bias)
    return pl.pallas_call(
        patch_kernel,
        out_shape=(pack, pack),
        in_specs=[pl.BlockSpec(memory_space=pltpu.HBM)] * 4,
        out_specs=(pl.BlockSpec(memory_space=pltpu.VMEM),) * 2,
        scratch_shapes=[pltpu.VMEM(value.shape, value.dtype) for value in operands]
        + [pltpu.SemaphoreType.DMA((4,))],
        name="patches",
        cost_estimate=pl.CostEstimate(
            flops=1_000_000_000, bytes_accessed=1_800_000, transcendentals=0
        ),
    )(*operands)


def frame_order(incoming):
    window = lax.broadcasted_iota(jnp.int32, (288, 1) if incoming else (1, 288), 0 if incoming else 1)
    source = lax.broadcasted_iota(jnp.int32, (288, 288), 1 if incoming else 0)
    pair, rest = window // 144, window % 144
    quad, rest = rest // 36, rest % 36
    level = (2 * pair + rest // 18 + 1) % 4
    place = level * 18 + rest % 18 if incoming else rest % 18 * 4 + level
    return jnp.where(source == quad * 72 + place, 1.0, 0.0).astype(BF16)


def main_kernel(
    p0, p1, a0, a1, a2, a3, b0, b1, b2, b3, gain_ref, bias_ref,
    o0, o1, o2, o3,
    patch_s, merge_s, qkv_s, out_s, proj_s, ctx_s, sems,
):
    core, lat = lax.axis_index("lon") % 2, lax.axis_index("lat")
    x, y = lat % 4, lat // 4
    for source, at in ((p0, 0), (p1, 144)):
        target = patch_s.at[pl.ds(at, 144), :]
        pltpu.make_async_copy(source, target, sems.at[0]).start()

    def scatter(kind, source, k, side):
        def part(base, rows, target, sem, first, width):
            spot = (y + STEPS[k] + 4) % 4 if side == 0 else (x + STEPS[k] + 4) % 4
            cols = pl.ds(side * width + first, 384)
            held = source.at[:, pl.ds(base, rows), :]
            place = target.at[spot, :, :, cols] if side == 0 else target.at[:, spot, :, cols]
            pltpu.make_async_copy(held, place, sems.at[sem]).start()

        if kind == 0:
            part(0, 96, merge_s, 1, 0, 384)
        elif kind == 1:
            for n in range(3):
                part(96 + n * 48, 48, qkv_s, 2, n * 384, 1152)
        else:
            part(240, 48, out_s, 3, 0, 384)

    own, other = (a0, a1, a2, a3), (b0, b1, b2, b3)
    for near_core in range(2):

        @pl.when(core == near_core)
        def _():
            for kind in range(3):
                for blocks, side in ((own, near_core), (other, 1 - near_core)):
                    for k in range(4):
                        scatter(kind, blocks[k], k, side)

    to_window = frame_order(True)
    pltpu.make_async_copy(patch_s, patch_s, sems.at[0]).wait()
    pltpu.make_async_copy(merge_s, merge_s, sems.at[1]).wait()
    coarse = dot(patch_s[...], merge_s[...].reshape(1536, 768)).astype(BF16)
    coarse = dot(to_window, coarse).astype(BF16)
    gain, bias = gain_ref[...].reshape(1, 768), bias_ref[...].reshape(1, 768)
    normed = normalize(coarse.astype(F32), gain, bias).astype(BF16)
    pltpu.make_async_copy(qkv_s, qkv_s, sems.at[2]).wait()
    for n in range(6):
        cols = slice(n * 384, (n + 1) * 384)
        proj_s[:, cols] = dot(normed, qkv_s[:, :, :, cols].reshape(768, 384)).astype(BF16)

    lane = lax.broadcasted_iota(jnp.int32, (1, 128), 1) // 32
    query = lax.broadcasted_iota(jnp.int32, (576, 1), 0) % 144
    key = lax.broadcasted_iota(jnp.int32, (1, 144), 1)
    wraps = lat == jnp.where(core == 0, 15, 0)
    row_apart = ((query // 72) != (key // 72)) & wraps
    level_apart = (query // 18 % 2) != (key // 18 % 2)
    low = F32(-1e30)
    for pair in range(2):
        rows = slice(pair * 144, (pair + 1) * 144)
        apart = (row_apart | level_apart) if pair == 1 else row_apart
        penalty = jnp.where(apart, low, 0.0)
        for g in range(6):
            q = proj_s[rows, g * 128 : (g + 1) * 128]
            k = proj_s[rows, 768 + g * 128 : 768 + (g + 1) * 128]
            v = proj_s[rows, 1536 + g * 128 : 1536 + (g + 1) * 128]
            stacked = jnp.concatenate(
                [jnp.where(lane == h, q, jnp.zeros_like(q)) for h in range(4)], axis=0
            )
            scores = lax.dot_general(
                stacked, k, (((1,), (1,)), ((), ())), preferred_element_type=F32
            )
            scores = scores * (32**-0.5) + penalty
            peak = jnp.max(scores, axis=-1, keepdims=True)
            weights = jnp.exp(scores - peak)
            total = jnp.sum(weights, axis=-1, keepdims=True)
            mixed = dot(weights.astype(BF16), v) / total
            picked = mixed[:144] * jnp.where(lane == 0, 1.0, 0.0)
            for h in range(1, 4):
                picked = jnp.where(lane == h, mixed[h * 144 : (h + 1) * 144], picked)
            ctx_s[rows, g * 128 : (g + 1) * 128] = picked.astype(BF16)

    pltpu.make_async_copy(out_s, out_s, sems.at[3]).wait()
    branch = dot(ctx_s[...], out_s[...].reshape(768, 768))
    result = (coarse.astype(F32) + branch).astype(BF16)
    result = dot(frame_order(False), result).astype(BF16)
    for ref, first, count in ((o0, 0, 18), (o1, 72, 18), (o2, 144, 18), (o3, 216, 18)):
        for place in range(count):
            at = first + place * 4
            ref[place] = result[at : at + 4]


def main(quads, own, other, gain, bias):
    any_space = pl.BlockSpec(memory_space=pl.ANY)
    vmem = pl.BlockSpec(memory_space=pltpu.VMEM)
    quad = jax.ShapeDtypeStruct((18, 4, 768), BF16)
    return pl.pallas_call(
        main_kernel,
        out_shape=(quad,) * 4,
        in_specs=[any_space] * 10 + [vmem] * 2,
        out_specs=(vmem,) * 4,
        scratch_shapes=[
            pltpu.VMEM((288, 1536), BF16),
            pltpu.VMEM((4, 4, 96, 768), BF16),
            pltpu.VMEM((4, 4, 48, 2304), BF16),
            pltpu.VMEM((4, 4, 48, 768), BF16),
            pltpu.VMEM((288, 2304), BF16),
            pltpu.VMEM((288, 768), BF16),
            pltpu.SemaphoreType.DMA((4,)),
        ],
        name="main",
        compiler_params=pltpu.CompilerParams(vmem_limit_bytes=32 * 1024 * 1024),
        cost_estimate=pl.CostEstimate(
            flops=5_000_000_000, bytes_accessed=9_000_000, transcendentals=2_000_000
        ),
    )(*quads, *own, *other, gain, bias)


def tiles(quad):
    return quad.reshape(3, 6, 4, 768)


def shards(
    fine_input,
    merge_gain,
    merge_bias,
    merge_weight,
    coarse_gain,
    coarse_bias,
    coarse_qkv,
    coarse_out,
):
    weights = (merge_weight, coarse_qkv, coarse_out)
    fine = fine_input.reshape(1152, 384)
    left, held = cut(fine, weights)
    block = lax.all_to_all(held, AXES, 0, 0, axis_index_groups=near_groups())
    left = moved(left, shift_pairs(-1, 0))
    own = [block] + [moved(block, far_pairs(step)) for step in (1, -1, 2)]
    near_rows, far_rows = patches(fine, left, merge_gain, merge_bias)
    far_rows = moved(far_rows, shift_pairs(0, -1))
    other = []
    for piece in own:
        other.append(moved(piece, swap_pairs()))
    result = main([near_rows, far_rows], own, other, coarse_gain, coarse_bias)
    near_left = moved(result[3], shift_pairs(-1, 1, back=True))
    far_right = moved(result[2], shift_pairs(0, -1, back=True))
    far_left = moved(result[1], shift_pairs(-1, 0, back=True))
    near = [tiles(near_left), tiles(result[0])]
    far = [tiles(far_left), tiles(far_right)]
    upper = lax.axis_index("lon") % 2 == 1
    above = jnp.concatenate([jnp.where(upper, a, b) for a, b in zip(near, far)], axis=1)
    below = jnp.concatenate([jnp.where(upper, b, a) for a, b in zip(near, far)], axis=1)
    return jnp.concatenate([above, below], axis=0).transpose(2, 0, 1, 3)


def solution(mesh):
    placed = (
        P(None, "lat", "lon", None),
        P(),
        P(),
        P("lat", None),
        P(),
        P(),
        P("lat", None),
        P("lat", None),
    )
    return jax.shard_map(
        shards, mesh=mesh, in_specs=placed, out_specs=P(None, "lat", "lon", None), check_vma=False
    )
```

profile of v0, /device:TPU:62, one launch (start us, length us, event | category | flops | bytes accessed | tf_op | source)
XLA Modules:
  0.0 109.6 jit_solution(1370318998552021382)
XLA Ops:
  0.0 3.2 %cut.1 = (bf16[576,384]{1,0:T(8,128)(2,1)}, bf16[4,288,384]{2,1,0:T(8,128)(2,1)}) custom-call(bf16[1152,384]{1,0:T(8,128)(2,1)} %bitcast.16, bf16[96,768]{1,0:T(8,128)(2,1)} %merge_hbm.1, bf16[48,2304]{1,0:T(8,128)(2,1)} %qkv_hbm.1, bf16[48,768]{1,0:T(8,128)(2,1)} %out_hbm.1), custom_call_target="tpu_custom_call" | custom-call | flops 1000000 | bytes 1800000 | tf_op jit(solution)/shard_map/cut/pallas_call | solution.py:119
  3.2 0.0 copy-start.3
  3.2 12.9 %all_to_all.5.a0 = bf16[4,288,384]{2,1,0:T(8,128)(2,1)S(1)} all-to-all(bf16[4,288,384]{2,1,0:T(8,128)(2,1)} %get-tuple-element.16), channel_id=1, replica_groups={{0,1,2,3},{4,5,6,7},{8,9,10,11},{12,13,14,15},{16,20,24,28},{17,21,25,2..., dimensions={0} | all-to-all | bytes 1769472 | tf_op jit(solution)/shard_map/all_to_all | solution.py:339
  16.0 6.2 %collective-permute-start.2 = (bf16[4,288,384]{2,1,0:T(8,128)(2,1)S(1)}, bf16[4,288,384]{2,1,0:T(8,128)(2,1)S(1)}, u32[]{:S(2)}, u32[]{:S(2)}) collective-permute-start(bf16[4,288,384]{2,1,0:T(8,128)(2,1)S(1)} %all_to_all.5.a0), channel_id=1, source_target_pairs={{0,4},{1,5},{2,6},{3,7},{4,8},{5,9},{6,10},{7,11},{8,12},{9,13},{1... | collective-permute-start | bytes 2654216 | tf_op jit(solution)/shard_map/ppermute | solution.py:70
  22.2 1.9 %collective-permute-start.3 = (bf16[4,288,384]{2,1,0:T(8,128)(2,1)S(1)}, bf16[4,288,384]{2,1,0:T(8,128)(2,1)S(1)}, u32[]{:S(2)}, u32[]{:S(2)}) collective-permute-start(bf16[4,288,384]{2,1,0:T(8,128)(2,1)S(1)} %all_to_all.5.a0), channel_id=1, source_target_pairs={{0,268},{1,269},{2,270},{3,271},{4,0},{5,1},{6,2},{7,3},{8,4},{9,5... | collective-permute-start | bytes 2654216 | tf_op jit(solution)/shard_map/ppermute | solution.py:70
  24.2 1.9 %collective-permute-start.4 = (bf16[4,288,384]{2,1,0:T(8,128)(2,1)S(1)}, bf16[4,288,384]{2,1,0:T(8,128)(2,1)}, u32[]{:S(2)}, u32[]{:S(2)}) collective-permute-start(bf16[4,288,384]{2,1,0:T(8,128)(2,1)S(1)} %all_to_all.5.a0), channel_id=1, source_target_pairs={{0,8},{1,9},{2,10},{3,11},{4,268},{5,269},{6,270},{7,271},{8,256},... | collective-permute-start | bytes 2654216 | tf_op jit(solution)/shard_map/ppermute | solution.py:70
  26.1 0.0 copy-start
  26.1 0.0 copy-start.1
  26.1 13.6 %collective-permute-start = (bf16[576,384]{1,0:T(8,128)(2,1)S(1)}, bf16[576,384]{1,0:T(8,128)(2,1)S(1)}, u32[]{:S(2)}, u32[]{:S(2)}) collective-permute-start(bf16[576,384]{1,0:T(8,128)(2,1)S(1)} %copy-done.3), channel_id=1, source_target_pairs={{0,496},{1,497},{2,498},{3,499},{4,500},{5,501},{6,502},{7,503},{8... | collective-permute-start | bytes 1327112 | tf_op jit(solution)/shard_map/ppermute | solution.py:70
  39.8 1.9 %collective-permute-start.5 = (bf16[4,288,384]{2,1,0:T(8,128)(2,1)S(1)}, bf16[4,288,384]{2,1,0:T(8,128)(2,1)}, u32[]{:S(2)}, u32[]{:S(2)}) collective-permute-start(bf16[4,288,384]{2,1,0:T(8,128)(2,1)S(1)} %all_to_all.5.a0), channel_id=1, source_target_pairs={{0,16},{1,17},{2,18},{3,19},{4,20},{5,21},{6,22},{7,23},{8,24},{9,... | collective-permute-start | bytes 2654216 | tf_op jit(solution)/shard_map/ppermute | solution.py:70
  41.7 9.8 %collective-permute-done.2.a1 = bf16[4,288,384]{2,1,0:T(8,128)(2,1)S(1)} collective-permute-done((bf16[4,288,384]{2,1,0:T(8,128)(2,1)S(1)}, bf16[4,288,384]{2,1,0:T(8,128)(2,1)S(1)}, u32[]{:S(2)}, u32[]{:S(2)}) %collective-permute-start.2) | collective-permute-done | bytes 884768 | tf_op jit(solution)/shard_map/ppermute | solution.py:70
  51.5 1.9 %collective-permute-start.6 = (bf16[4,288,384]{2,1,0:T(8,128)(2,1)S(1)}, bf16[4,288,384]{2,1,0:T(8,128)(2,1)}, u32[]{:S(2)}, u32[]{:S(2)}) collective-permute-start(bf16[4,288,384]{2,1,0:T(8,128)(2,1)S(1)} %collective-permute-done.2.a1), channel_id=1, source_target_pairs={{0,16},{1,17},{2,18},{3,19},{4,20},{5,21},{6,22},{7,23},{8,24},{9,... | collective-permute-start | bytes 2654216 | tf_op jit(solution)/shard_map/ppermute | solution.py:70
  53.4 4.0 %collective-permute-done.3.a2 = bf16[4,288,384]{2,1,0:T(8,128)(2,1)S(1)} collective-permute-done((bf16[4,288,384]{2,1,0:T(8,128)(2,1)S(1)}, bf16[4,288,384]{2,1,0:T(8,128)(2,1)S(1)}, u32[]{:S(2)}, u32[]{:S(2)}) %collective-permute-start.3) | collective-permute-done | bytes 884768 | tf_op jit(solution)/shard_map/ppermute | solution.py:70
  57.3 1.9 %collective-permute-start.7 = (bf16[4,288,384]{2,1,0:T(8,128)(2,1)S(1)}, bf16[4,288,384]{2,1,0:T(8,128)(2,1)}, u32[]{:S(2)}, u32[]{:S(2)}) collective-permute-start(bf16[4,288,384]{2,1,0:T(8,128)(2,1)S(1)} %collective-permute-done.3.a2), channel_id=1, source_target_pairs={{0,16},{1,17},{2,18},{3,19},{4,20},{5,21},{6,22},{7,23},{8,24},{9,... | collective-permute-start | bytes 2654216 | tf_op jit(solution)/shard_map/ppermute | solution.py:70
  59.3 0.0 collective-permute-done.4.a3
  59.3 2.4 %collective-permute-start.8 = (bf16[4,288,384]{2,1,0:T(8,128)(2,1)}, bf16[4,288,384]{2,1,0:T(8,128)(2,1)}, u32[]{:S(2)}, u32[]{:S(2)}) collective-permute-start(bf16[4,288,384]{2,1,0:T(8,128)(2,1)} %collective-permute-done.4.a3), channel_id=1, source_target_pairs={{0,16},{1,17},{2,18},{3,19},{4,20},{5,21},{6,22},{7,23},{8,24},{9,... | collective-permute-start | bytes 2654216 | tf_op jit(solution)/shard_map/ppermute | solution.py:70
  61.7 0.0 collective-permute-done.left_hbm
  61.7 0.0 copy-start.4
  61.7 0.8 copy-done.4
  62.5 4.1 %patches.1 = (bf16[144,1536]{1,0:T(8,128)(2,1)}, bf16[144,1536]{1,0:T(8,128)(2,1)}) custom-call(bf16[1152,384]{1,0:T(8,128)(2,1)} %bitcast.17, bf16[576,384]{1,0:T(8,128)(2,1)} %copy-done.4, f32[1536]{0:T(1024)} %gain_hbm.1, f32[1536]{0:T(1024)} %bias_hbm.1), custom_call_target="tpu_custom_call" | custom-call | flops 1000000000 | bytes 1800000 | tf_op jit(solution)/shard_map/patches/pallas_call | solution.py:182
  66.5 2.2 %collective-permute-start.1 = (bf16[144,1536]{1,0:T(8,128)(2,1)}, bf16[144,1536]{1,0:T(8,128)(2,1)S(1)}, u32[]{:S(2)}, u32[]{:S(2)}) collective-permute-start(bf16[144,1536]{1,0:T(8,128)(2,1)} %get-tuple-element.15), channel_id=1, source_target_pairs={{0,15},{1,0},{2,1},{3,2},{4,3},{5,4},{6,5},{7,6},{8,7},{9,8},{10,9... | collective-permute-start | bytes 1327112 | tf_op jit(solution)/shard_map/ppermute | solution.py:70
  68.8 12.1 %collective-permute-done.1.p1 = bf16[144,1536]{1,0:T(8,128)(2,1)S(1)} collective-permute-done((bf16[144,1536]{1,0:T(8,128)(2,1)}, bf16[144,1536]{1,0:T(8,128)(2,1)S(1)}, u32[]{:S(2)}, u32[]{:S(2)}) %collective-permute-start.1) | collective-permute-done | bytes 442400 | tf_op jit(solution)/shard_map/ppermute | solution.py:70
  80.9 0.0 collective-permute-done.8.b3
  80.9 1.0 copy-done.2
  81.9 9.1 %main.1 = (bf16[18,4,768]{2,1,0:T(4,128)(2,1)S(1)}, bf16[18,4,768]{2,1,0:T(4,128)(2,1)S(1)}, bf16[18,4,768]{2,1,0:T(4,128)(2,1)S(1)}, bf16[18,4,768]{2,1,0:T(4,128)(2,1)S(1)}) custom-call(bf16[144,1536]{1,0:T(8,128)(2,1)S(1)} %copy-done.2, bf16[144,1536]{1,0:T(8,128)(2,1)S(1)} %collective-permute-done.1.p1, bf16[4,288,384]{2,1,0:T(8,128)(2,1)S(1)} %all_to_all.5.a0, ...), custom_call_target="tpu_custom_call" | custom-call | flops 5000000000 | bytes 9000000 | tf_op jit(solution)/shard_map/main/pallas_call | solution.py:300
  91.1 1.9 %collective-permute-start.11 = (bf16[18,4,768]{2,1,0:T(4,128)(2,1)S(1)}, bf16[18,4,768]{2,1,0:T(4,128)(2,1)S(1)}, u32[]{:S(2)}, u32[]{:S(2)}) collective-permute-start(bf16[18,4,768]{2,1,0:T(4,128)(2,1)S(1)} %get-tuple-element.20), channel_id=1, source_target_pairs={{15,0},{0,1},{1,2},{2,3},{3,4},{4,5},{5,6},{6,7},{7,8},{8,9},{9,10... | collective-permute-start | bytes 331784 | tf_op jit(solution)/shard_map/ppermute | solution.py:70
  93.0 2.1 %collective-permute-start.9 = (bf16[18,4,768]{2,1,0:T(4,128)(2,1)S(1)}, bf16[18,4,768]{2,1,0:T(4,128)(2,1)S(1)}, u32[]{:S(2)}, u32[]{:S(2)}) collective-permute-start(bf16[18,4,768]{2,1,0:T(4,128)(2,1)S(1)} %get-tuple-element.17), channel_id=1, source_target_pairs={{497,0},{498,1},{499,2},{500,3},{501,4},{502,5},{503,6},{504,7},{5... | collective-permute-start | bytes 331784 | tf_op jit(solution)/shard_map/ppermute | solution.py:70
  95.1 1.9 %collective-permute-start.10 = (bf16[18,4,768]{2,1,0:T(4,128)(2,1)S(1)}, bf16[18,4,768]{2,1,0:T(4,128)(2,1)S(1)}, u32[]{:S(2)}, u32[]{:S(2)}) collective-permute-start(bf16[18,4,768]{2,1,0:T(4,128)(2,1)S(1)} %get-tuple-element.18), channel_id=1, source_target_pairs={{496,0},{497,1},{498,2},{499,3},{500,4},{501,5},{502,6},{503,7},{5... | collective-permute-start | bytes 331784 | tf_op jit(solution)/shard_map/ppermute | solution.py:70
  97.0 0.7 collective-permute-done.11
  97.7 6.8 %collective-permute-done.9 = bf16[18,4,768]{2,1,0:T(4,128)(2,1)S(1)} collective-permute-done((bf16[18,4,768]{2,1,0:T(4,128)(2,1)S(1)}, bf16[18,4,768]{2,1,0:T(4,128)(2,1)S(1)}, u32[]{:S(2)}, u32[]{:S(2)}) %collective-permute-start.9) | collective-permute-done | bytes 110624 | tf_op jit(solution)/shard_map/ppermute | solution.py:70
  104.5 4.0 %collective-permute-done.10 = bf16[18,4,768]{2,1,0:T(4,128)(2,1)S(1)} collective-permute-done((bf16[18,4,768]{2,1,0:T(4,128)(2,1)S(1)}, bf16[18,4,768]{2,1,0:T(4,128)(2,1)S(1)}, u32[]{:S(2)}, u32[]{:S(2)}) %collective-permute-start.10) | collective-permute-done | bytes 110624 | tf_op jit(solution)/shard_map/ppermute | solution.py:70
  108.5 1.1 maximum_bitcast_fusion
  (9 shorter events, 0.1 us)
Async XLA Ops:
  3.2 22.9 %copy-start.3 = (bf16[576,384]{1,0:T(8,128)(2,1)S(1)}, bf16[576,384]{1,0:T(8,128)(2,1)}, u32[]{:S(2)}) copy-start(bf16[576,384]{1,0:T(8,128)(2,1)} %get-tuple-element.13) | copy-start | bytes 1327108
  16.0 35.4 %collective-permute-start.2 = (bf16[4,288,384]{2,1,0:T(8,128)(2,1)S(1)}, bf16[4,288,384]{2,1,0:T(8,128)(2,1)S(1)}, u32[]{:S(2)}, u32[]{:S(2)}) collective-permute-start(bf16[4,288,384]{2,1,0:T(8,128)(2,1)S(1)} %all_to_all.5.a0), channel_id=1, source_target_pairs={{0,4},{1,5},{2,6},{3,7},{4,8},{5,9},{6,10},{7,11},{8,12},{9,13},{1... | collective-permute-start | bytes 2654216 | tf_op jit(solution)/shard_map/ppermute | solution.py:70
  22.2 35.1 %collective-permute-start.3 = (bf16[4,288,384]{2,1,0:T(8,128)(2,1)S(1)}, bf16[4,288,384]{2,1,0:T(8,128)(2,1)S(1)}, u32[]{:S(2)}, u32[]{:S(2)}) collective-permute-start(bf16[4,288,384]{2,1,0:T(8,128)(2,1)S(1)} %all_to_all.5.a0), channel_id=1, source_target_pairs={{0,268},{1,269},{2,270},{3,271},{4,0},{5,1},{6,2},{7,3},{8,4},{9,5... | collective-permute-start | bytes 2654216 | tf_op jit(solution)/shard_map/ppermute | solution.py:70
  24.2 35.1 %collective-permute-start.4 = (bf16[4,288,384]{2,1,0:T(8,128)(2,1)S(1)}, bf16[4,288,384]{2,1,0:T(8,128)(2,1)}, u32[]{:S(2)}, u32[]{:S(2)}) collective-permute-start(bf16[4,288,384]{2,1,0:T(8,128)(2,1)S(1)} %all_to_all.5.a0), channel_id=1, source_target_pairs={{0,8},{1,9},{2,10},{3,11},{4,268},{5,269},{6,270},{7,271},{8,256},... | collective-permute-start | bytes 2654216 | tf_op jit(solution)/shard_map/ppermute | solution.py:70
  26.1 54.8 %copy-start = (f32[768]{0:T(1024)S(1)}, f32[768]{0:T(1024)}, u32[]{:S(2)}) copy-start(f32[768]{0:T(1024)} %gain_ref.1) | copy-start | bytes 9220
  26.1 54.8 %copy-start.1 = (f32[768]{0:T(1024)S(1)}, f32[768]{0:T(1024)}, u32[]{:S(2)}) copy-start(f32[768]{0:T(1024)} %bias_ref.1) | copy-start | bytes 9220
  26.1 35.6 %collective-permute-start = (bf16[576,384]{1,0:T(8,128)(2,1)S(1)}, bf16[576,384]{1,0:T(8,128)(2,1)S(1)}, u32[]{:S(2)}, u32[]{:S(2)}) collective-permute-start(bf16[576,384]{1,0:T(8,128)(2,1)S(1)} %copy-done.3), channel_id=1, source_target_pairs={{0,496},{1,497},{2,498},{3,499},{4,500},{5,501},{6,502},{7,503},{8... | collective-permute-start | bytes 1327112 | tf_op jit(solution)/shard_map/ppermute | solution.py:70
  39.8 41.1 %collective-permute-start.5 = (bf16[4,288,384]{2,1,0:T(8,128)(2,1)S(1)}, bf16[4,288,384]{2,1,0:T(8,128)(2,1)}, u32[]{:S(2)}, u32[]{:S(2)}) collective-permute-start(bf16[4,288,384]{2,1,0:T(8,128)(2,1)S(1)} %all_to_all.5.a0), channel_id=1, source_target_pairs={{0,16},{1,17},{2,18},{3,19},{4,20},{5,21},{6,22},{7,23},{8,24},{9,... | collective-permute-start | bytes 2654216 | tf_op jit(solution)/shard_map/ppermute | solution.py:70
  51.5 29.4 %collective-permute-start.6 = (bf16[4,288,384]{2,1,0:T(8,128)(2,1)S(1)}, bf16[4,288,384]{2,1,0:T(8,128)(2,1)}, u32[]{:S(2)}, u32[]{:S(2)}) collective-permute-start(bf16[4,288,384]{2,1,0:T(8,128)(2,1)S(1)} %collective-permute-done.2.a1), channel_id=1, source_target_pairs={{0,16},{1,17},{2,18},{3,19},{4,20},{5,21},{6,22},{7,23},{8,24},{9,... | collective-permute-start | bytes 2654216 | tf_op jit(solution)/shard_map/ppermute | solution.py:70
  57.3 23.5 %collective-permute-start.7 = (bf16[4,288,384]{2,1,0:T(8,128)(2,1)S(1)}, bf16[4,288,384]{2,1,0:T(8,128)(2,1)}, u32[]{:S(2)}, u32[]{:S(2)}) collective-permute-start(bf16[4,288,384]{2,1,0:T(8,128)(2,1)S(1)} %collective-permute-done.3.a2), channel_id=1, source_target_pairs={{0,16},{1,17},{2,18},{3,19},{4,20},{5,21},{6,22},{7,23},{8,24},{9,... | collective-permute-start | bytes 2654216 | tf_op jit(solution)/shard_map/ppermute | solution.py:70
  59.3 21.6 %collective-permute-start.8 = (bf16[4,288,384]{2,1,0:T(8,128)(2,1)}, bf16[4,288,384]{2,1,0:T(8,128)(2,1)}, u32[]{:S(2)}, u32[]{:S(2)}) collective-permute-start(bf16[4,288,384]{2,1,0:T(8,128)(2,1)} %collective-permute-done.4.a3), channel_id=1, source_target_pairs={{0,16},{1,17},{2,18},{3,19},{4,20},{5,21},{6,22},{7,23},{8,24},{9,... | collective-permute-start | bytes 2654216 | tf_op jit(solution)/shard_map/ppermute | solution.py:70
  61.7 0.8 copy-start.4
  66.5 14.3 %collective-permute-start.1 = (bf16[144,1536]{1,0:T(8,128)(2,1)}, bf16[144,1536]{1,0:T(8,128)(2,1)S(1)}, u32[]{:S(2)}, u32[]{:S(2)}) collective-permute-start(bf16[144,1536]{1,0:T(8,128)(2,1)} %get-tuple-element.15), channel_id=1, source_target_pairs={{0,15},{1,0},{2,1},{3,2},{4,3},{5,4},{6,5},{7,6},{8,7},{9,8},{10,9... | collective-permute-start | bytes 1327112 | tf_op jit(solution)/shard_map/ppermute | solution.py:70
  80.9 1.0 copy-start.2
  91.1 6.6 %collective-permute-start.11 = (bf16[18,4,768]{2,1,0:T(4,128)(2,1)S(1)}, bf16[18,4,768]{2,1,0:T(4,128)(2,1)S(1)}, u32[]{:S(2)}, u32[]{:S(2)}) collective-permute-start(bf16[18,4,768]{2,1,0:T(4,128)(2,1)S(1)} %get-tuple-element.20), channel_id=1, source_target_pairs={{15,0},{0,1},{1,2},{2,3},{3,4},{4,5},{5,6},{6,7},{7,8},{8,9},{9,10... | collective-permute-start | bytes 331784 | tf_op jit(solution)/shard_map/ppermute | solution.py:70
  93.0 11.5 %collective-permute-start.9 = (bf16[18,4,768]{2,1,0:T(4,128)(2,1)S(1)}, bf16[18,4,768]{2,1,0:T(4,128)(2,1)S(1)}, u32[]{:S(2)}, u32[]{:S(2)}) collective-permute-start(bf16[18,4,768]{2,1,0:T(4,128)(2,1)S(1)} %get-tuple-element.17), channel_id=1, source_target_pairs={{497,0},{498,1},{499,2},{500,3},{501,4},{502,5},{503,6},{504,7},{5... | collective-permute-start | bytes 331784 | tf_op jit(solution)/shard_map/ppermute | solution.py:70
  95.1 13.4 %collective-permute-start.10 = (bf16[18,4,768]{2,1,0:T(4,128)(2,1)S(1)}, bf16[18,4,768]{2,1,0:T(4,128)(2,1)S(1)}, u32[]{:S(2)}, u32[]{:S(2)}) collective-permute-start(bf16[18,4,768]{2,1,0:T(4,128)(2,1)S(1)} %get-tuple-element.18), channel_id=1, source_target_pairs={{496,0},{497,1},{498,2},{499,3},{500,4},{501,5},{502,6},{503,7},{5... | collective-permute-start | bytes 331784 | tf_op jit(solution)/shard_map/ppermute | solution.py:70
where the time goes:
time: 110 us
  starting transfers between devices  40 us (36%)
  waiting for transfers between devices  37.2 us (34%)
  Pallas kernels  16.4 us (15%)
  blocking collectives  12.9 us (12%)
  local copies, waits for them, and re-layouts  1.78 us (2%)
  other arithmetic  1.12 us (1%)
    ppermute x12, starting transfers between devices, moved(): return lax.ppermute(value, AXES, pairs)  40 us
    ppermute x12, waiting for transfers between devices, moved(): return lax.ppermute(value, AXES, pairs)  37.2 us
    all_to_all x1, blocking collectives, shards(): block = lax.all_to_all(held, AXES, 0, 0, axis_index_groups=near_groups())  12.9 us
    pallas_call x1, Pallas kernels, main(): pl.pallas_call(main_kernel, out_shape=(quad,) * 4, in_specs=[any_space] *...  9.15 us
    pallas_call x1, Pallas kernels, patches(): pl.pallas_call(patch_kernel, out_shape=(pack, pack), in_specs=[pl.BlockSp...  4.06 us
    pallas_call x1, Pallas kernels, cut(): pl.pallas_call(cut_kernel, out_shape=(jax.ShapeDtypeStruct((576, 384), BF...  3.16 us
  transfers between devices with their start and end apart: 12, of which 6 were waited for; matrix products, arithmetic and copies ran while one was open for 0% of the time, Pallas kernels for 4%

commit v1 on v0

--- a/solution.py
+++ b/solution.py
@@ -84,14 +84,14 @@
     return centered * lax.rsqrt(spread + EPSILON) * gain + bias
 
 
-def cut_kernel(fine_ref, merge_hbm, qkv_hbm, out_hbm, left_ref, held_hbm, sems):
+def cut_kernel(merge_ref, qkv_ref, out_ref, held_hbm, sems):
     core = lax.axis_index("lon") % 2
     for side in range(2):
 
         @pl.when(core == side)
         def _():
-            cuts = [(merge_hbm, side * 384, 0, 96), (out_hbm, side * 384, 240, 48)]
-            cuts += [(qkv_hbm, side * 1152 + n * 384, 96 + n * 48, 48) for n in range(3)]
+            cuts = [(merge_ref, side * 384, 0, 96), (out_ref, side * 384, 240, 48)]
+            cuts += [(qkv_ref, side * 1152 + n * 384, 96 + n * 48, 48) for n in range(3)]
             copies = []
             for member in range(4):
                 for n, (source, column, row, rows) in enumerate(cuts):
@@ -104,30 +104,40 @@
                     )
             for copy in copies:
                 copy.start()
-            row = lax.broadcasted_iota(jnp.int32, (144, 1), 0)
-            source = lax.broadcasted_iota(jnp.int32, (144, 288), 1)
-            pick = jnp.where(source == row // 12 * 24 + row % 12, 1.0, 0.0).astype(BF16)
-            for level in range(4):
-                part = dot(pick, fine_ref[level * 288 : level * 288 + 288])
-                left_ref[level * 144 : level * 144 + 144] = part.astype(BF16)
             for copy in copies:
                 copy.wait()
 
 
-def cut(fine, weights):
-    vmem = pl.BlockSpec(memory_space=pltpu.VMEM)
+def cut(weights):
     return pl.pallas_call(
         cut_kernel,
-        out_shape=(
-            jax.ShapeDtypeStruct((576, 384), BF16),
-            jax.ShapeDtypeStruct((4, 288, 384), BF16),
-        ),
-        in_specs=[vmem] * 4,
-        out_specs=(vmem, vmem),
+        out_shape=jax.ShapeDtypeStruct((4, 288, 384), BF16),
+        in_specs=[pl.BlockSpec(memory_space=pltpu.VMEM)] * 3,
+        out_specs=pl.BlockSpec(memory_space=pl.ANY),
         scratch_shapes=[pltpu.SemaphoreType.DMA((20,))],
         name="cut",
         cost_estimate=pl.CostEstimate(flops=1_000_000, bytes_accessed=1_800_000, transcendentals=0),
-    )(fine, *weights)
+    )(*weights)
+
+
+def left_kernel(fine_ref, left_ref):
+    row = lax.broadcasted_iota(jnp.int32, (144, 1), 0)
+    source = lax.broadcasted_iota(jnp.int32, (144, 288), 1)
+    pick = jnp.where(source == row // 12 * 24 + row % 12, 1.0, 0.0).astype(BF16)
+    for level in range(4):
+        part = dot(pick, fine_ref[level * 288 : level * 288 + 288])
+        left_ref[level * 144 : level * 144 + 144] = part.astype(BF16)
+
+
+def left_half(fine):
+    return pl.pallas_call(
+        left_kernel,
+        out_shape=jax.ShapeDtypeStruct((576, 384), BF16),
+        name="left",
+        cost_estimate=pl.CostEstimate(
+            flops=200_000_000, bytes_accessed=1_400_000, transcendentals=0
+        ),
+    )(fine)
 
 
 def patch_kernel(
@@ -187,6 +197,7 @@
         scratch_shapes=[pltpu.VMEM(value.shape, value.dtype) for value in operands]
         + [pltpu.SemaphoreType.DMA((4,))],
         name="patches",
+        compiler_params=pltpu.CompilerParams(vmem_limit_bytes=12 * 1024 * 1024),
         cost_estimate=pl.CostEstimate(
             flops=1_000_000_000, bytes_accessed=1_800_000, transcendentals=0
         ),
@@ -312,7 +323,7 @@
             pltpu.SemaphoreType.DMA((4,)),
         ],
         name="main",
-        compiler_params=pltpu.CompilerParams(vmem_limit_bytes=32 * 1024 * 1024),
+        compiler_params=pltpu.CompilerParams(vmem_limit_bytes=20 * 1024 * 1024),
         cost_estimate=pl.CostEstimate(
             flops=5_000_000_000, bytes_accessed=9_000_000, transcendentals=2_000_000
         ),
@@ -335,8 +346,8 @@
 ):
     weights = (merge_weight, coarse_qkv, coarse_out)
     fine = fine_input.reshape(1152, 384)
-    left, held = cut(fine, weights)
-    block = lax.all_to_all(held, AXES, 0, 0, axis_index_groups=near_groups())
+    block = lax.all_to_all(cut(weights), AXES, 0, 0, axis_index_groups=near_groups())
+    left = left_half(fine)
     left = moved(left, shift_pairs(-1, 0))
     own = [block] + [moved(block, far_pairs(step)) for step in (1, -1, 2)]
     near_rows, far_rows = patches(fine, left, merge_gain, merge_bias)

time: 110 us -> 104 us (0.945)
  the two profiles are of different devices: /device:TPU:62 before, /device:TPU:30 now
where the time goes in v1:
time: 104 us
  starting transfers between devices  42.3 us (41%)
  waiting for transfers between devices  30.9 us (30%)
  Pallas kernels  16.3 us (16%)
  blocking collectives  12.7 us (12%)
  other arithmetic  1.13 us (1%)
    ppermute x12, starting transfers between devices, moved(): return lax.ppermute(value, AXES, pairs)  42.3 us
    ppermute x12, waiting for transfers between devices, moved(): return lax.ppermute(value, AXES, pairs)  30.9 us
    all_to_all x1, blocking collectives, shards(): lax.all_to_all(cut(weights), AXES, 0, 0, axis_index_groups=near_groups())  12.7 us
    pallas_call x1, Pallas kernels, main(): pl.pallas_call(main_kernel, out_shape=(quad,) * 4, in_specs=[any_space] *...  9.18 us
    pallas_call x1, Pallas kernels, patches(): pl.pallas_call(patch_kernel, out_shape=(pack, pack), in_specs=[pl.BlockSp...  2.55 us
    pallas_call x1, Pallas kernels, left_half(): pl.pallas_call(left_kernel, out_shape=jax.ShapeDtypeStruct((576, 384), BF...  2.4 us
    pallas_call x1, Pallas kernels, cut(): pl.pallas_call(cut_kernel, out_shape=jax.ShapeDtypeStruct((4, 288, 384),...  2.16 us
  transfers between devices with their start and end apart: 12, of which 5 were waited for; matrix products, arithmetic and copies ran while one was open for 0% of the time, Pallas kernels for 5%

profile of v1, /device:TPU:30, one launch (start us, length us, event | category | flops | bytes accessed | tf_op | source)
XLA Modules:
  0.0 103.6 jit_solution(5095305024001767600)
XLA Ops:
  0.0 2.2 %cut.1 = bf16[4,288,384]{2,1,0:T(8,128)(2,1)} custom-call(bf16[96,768]{1,0:T(8,128)(2,1)} %merge_ref.1, bf16[48,2304]{1,0:T(8,128)(2,1)} %qkv_ref.1, bf16[48,768]{1,0:T(8,128)(2,1)} %out_ref.1), custom_call_target="tpu_custom_call" | custom-call | flops 1000000 | bytes 1800000 | tf_op jit(solution)/shard_map/cut/pallas_call | solution.py:112
  2.2 12.7 %all_to_all.5.a0 = bf16[4,288,384]{2,1,0:T(8,128)(2,1)S(1)} all-to-all(bf16[4,288,384]{2,1,0:T(8,128)(2,1)} %cut.1), channel_id=1, replica_groups={{0,1,2,3},{4,5,6,7},{8,9,10,11},{12,13,14,15},{16,20,24,28},{17,21,25,2..., dimensions={0} | all-to-all | bytes 1769472 | tf_op jit(solution)/shard_map/all_to_all | solution.py:349
  14.9 4.8 %collective-permute-start.2 = (bf16[4,288,384]{2,1,0:T(8,128)(2,1)S(1)}, bf16[4,288,384]{2,1,0:T(8,128)(2,1)S(1)}, u32[]{:S(2)}, u32[]{:S(2)}) collective-permute-start(bf16[4,288,384]{2,1,0:T(8,128)(2,1)S(1)} %all_to_all.5.a0), channel_id=1, source_target_pairs={{0,4},{1,5},{2,6},{3,7},{4,8},{5,9},{6,10},{7,11},{8,12},{9,13},{1... | collective-permute-start | bytes 2654216 | tf_op jit(solution)/shard_map/ppermute | solution.py:70
  19.7 1.9 %collective-permute-start.3 = (bf16[4,288,384]{2,1,0:T(8,128)(2,1)S(1)}, bf16[4,288,384]{2,1,0:T(8,128)(2,1)S(1)}, u32[]{:S(2)}, u32[]{:S(2)}) collective-permute-start(bf16[4,288,384]{2,1,0:T(8,128)(2,1)S(1)} %all_to_all.5.a0), channel_id=1, source_target_pairs={{0,268},{1,269},{2,270},{3,271},{4,0},{5,1},{6,2},{7,3},{8,4},{9,5... | collective-permute-start | bytes 2654216 | tf_op jit(solution)/shard_map/ppermute | solution.py:70
  21.7 4.4 %collective-permute-start.4 = (bf16[4,288,384]{2,1,0:T(8,128)(2,1)S(1)}, bf16[4,288,384]{2,1,0:T(8,128)(2,1)}, u32[]{:S(2)}, u32[]{:S(2)}) collective-permute-start(bf16[4,288,384]{2,1,0:T(8,128)(2,1)S(1)} %all_to_all.5.a0), channel_id=1, source_target_pairs={{0,8},{1,9},{2,10},{3,11},{4,268},{5,269},{6,270},{7,271},{8,256},... | collective-permute-start | bytes 2654216 | tf_op jit(solution)/shard_map/ppermute | solution.py:70
  26.1 0.0 copy-start.1
  26.1 0.0 copy-start.2
  26.1 2.4 %left.1 = bf16[576,384]{1,0:T(8,128)(2,1)} custom-call(bf16[1152,384]{1,0:T(8,128)(2,1)} %bitcast.15), custom_call_target="tpu_custom_call" | custom-call | flops 200000000 | bytes 1400000 | tf_op jit(solution)/shard_map/left/pallas_call | solution.py:133
  28.5 14.7 %collective-permute-start = (bf16[576,384]{1,0:T(8,128)(2,1)}, bf16[576,384]{1,0:T(8,128)(2,1)S(1)}, u32[]{:S(2)}, u32[]{:S(2)}) collective-permute-start(bf16[576,384]{1,0:T(8,128)(2,1)} %left.1), channel_id=1, source_target_pairs={{0,496},{1,497},{2,498},{3,499},{4,500},{5,501},{6,502},{7,503},{8... | collective-permute-start | bytes 1327112 | tf_op jit(solution)/shard_map/ppermute | solution.py:70
  43.2 1.9 %collective-permute-start.5 = (bf16[4,288,384]{2,1,0:T(8,128)(2,1)S(1)}, bf16[4,288,384]{2,1,0:T(8,128)(2,1)S(1)}, u32[]{:S(2)}, u32[]{:S(2)}) collective-permute-start(bf16[4,288,384]{2,1,0:T(8,128)(2,1)S(1)} %all_to_all.5.a0), channel_id=1, source_target_pairs={{0,16},{1,17},{2,18},{3,19},{4,20},{5,21},{6,22},{7,23},{8,24},{9,... | collective-permute-start | bytes 2654216 | tf_op jit(solution)/shard_map/ppermute | solution.py:70
  45.1 0.0 collective-permute-done.2.a1
  45.1 2.4 %collective-permute-start.6 = (bf16[4,288,384]{2,1,0:T(8,128)(2,1)S(1)}, bf16[4,288,384]{2,1,0:T(8,128)(2,1)S(1)}, u32[]{:S(2)}, u32[]{:S(2)}) collective-permute-start(bf16[4,288,384]{2,1,0:T(8,128)(2,1)S(1)} %collective-permute-done.2.a1), channel_id=1, source_target_pairs={{0,16},{1,17},{2,18},{3,19},{4,20},{5,21},{6,22},{7,23},{8,24},{9,... | collective-permute-start | bytes 2654216 | tf_op jit(solution)/shard_map/ppermute | solution.py:70
  47.5 7.3 %collective-permute-done.3.a2 = bf16[4,288,384]{2,1,0:T(8,128)(2,1)S(1)} collective-permute-done((bf16[4,288,384]{2,1,0:T(8,128)(2,1)S(1)}, bf16[4,288,384]{2,1,0:T(8,128)(2,1)S(1)}, u32[]{:S(2)}, u32[]{:S(2)}) %collective-permute-start.3) | collective-permute-done | bytes 884768 | tf_op jit(solution)/shard_map/ppermute | solution.py:70
  54.8 1.9 %collective-permute-start.7 = (bf16[4,288,384]{2,1,0:T(8,128)(2,1)S(1)}, bf16[4,288,384]{2,1,0:T(8,128)(2,1)S(1)}, u32[]{:S(2)}, u32[]{:S(2)}) collective-permute-start(bf16[4,288,384]{2,1,0:T(8,128)(2,1)S(1)} %collective-permute-done.3.a2), channel_id=1, source_target_pairs={{0,16},{1,17},{2,18},{3,19},{4,20},{5,21},{6,22},{7,23},{8,24},{9,... | collective-permute-start | bytes 2654216 | tf_op jit(solution)/shard_map/ppermute | solution.py:70
  56.7 0.0 collective-permute-done.4.a3
  56.8 2.4 %collective-permute-start.8 = (bf16[4,288,384]{2,1,0:T(8,128)(2,1)}, bf16[4,288,384]{2,1,0:T(8,128)(2,1)S(1)}, u32[]{:S(2)}, u32[]{:S(2)}) collective-permute-start(bf16[4,288,384]{2,1,0:T(8,128)(2,1)} %collective-permute-done.4.a3), channel_id=1, source_target_pairs={{0,16},{1,17},{2,18},{3,19},{4,20},{5,21},{6,22},{7,23},{8,24},{9,... | collective-permute-start | bytes 2654216 | tf_op jit(solution)/shard_map/ppermute | solution.py:70
  59.2 0.0 collective-permute-done.left_hbm
  59.2 2.6 %patches.1 = (bf16[144,1536]{1,0:T(8,128)(2,1)S(1)}, bf16[144,1536]{1,0:T(8,128)(2,1)S(1)}) custom-call(bf16[1152,384]{1,0:T(8,128)(2,1)S(1)} %bitcast.16, bf16[576,384]{1,0:T(8,128)(2,1)S(1)} %collective-permute-done.left_hbm, f32[1536]{0:T(1024)S(1)} %copy-done.1, f32[1536]{0:T(1024)S(1)} %copy-done.2), custom_call_target="tpu_custom_call" | custom-call | flops 1000000000 | bytes 1800000 | tf_op jit(solution)/shard_map/patches/pallas_call | solution.py:192
  61.8 1.9 %collective-permute-start.1 = (bf16[144,1536]{1,0:T(8,128)(2,1)S(1)}, bf16[144,1536]{1,0:T(8,128)(2,1)S(1)}, u32[]{:S(2)}, u32[]{:S(2)}) collective-permute-start(bf16[144,1536]{1,0:T(8,128)(2,1)S(1)} %get-tuple-element.12), channel_id=1, source_target_pairs={{0,15},{1,0},{2,1},{3,2},{4,3},{5,4},{6,5},{7,6},{8,7},{9,8},{10,9... | collective-permute-start | bytes 1327112 | tf_op jit(solution)/shard_map/ppermute | solution.py:70
  63.7 12.2 %collective-permute-done.1.p1 = bf16[144,1536]{1,0:T(8,128)(2,1)S(1)} collective-permute-done((bf16[144,1536]{1,0:T(8,128)(2,1)S(1)}, bf16[144,1536]{1,0:T(8,128)(2,1)S(1)}, u32[]{:S(2)}, u32[]{:S(2)}) %collective-permute-start.1) | collective-permute-done | bytes 442400 | tf_op jit(solution)/shard_map/ppermute | solution.py:70
  75.9 0.0 collective-permute-done.5.b0
  75.9 0.0 collective-permute-done.6.b1
  75.9 0.0 collective-permute-done.7.b2
  75.9 0.0 collective-permute-done.8.b3
  75.9 9.2 %main.1 = (bf16[18,4,768]{2,1,0:T(4,128)(2,1)S(1)}, bf16[18,4,768]{2,1,0:T(4,128)(2,1)S(1)}, bf16[18,4,768]{2,1,0:T(4,128)(2,1)S(1)}, bf16[18,4,768]{2,1,0:T(4,128)(2,1)S(1)}) custom-call(bf16[144,1536]{1,0:T(8,128)(2,1)S(1)} %get-tuple-element.11.p0, bf16[144,1536]{1,0:T(8,128)(2,1)S(1)} %collective-permute-done.1.p1, ...), custom_call_target="tpu_custom_call" | custom-call | flops 5000000000 | bytes 9000000 | tf_op jit(solution)/shard_map/main/pallas_call | solution.py:311
  85.1 1.9 %collective-permute-start.11 = (bf16[18,4,768]{2,1,0:T(4,128)(2,1)S(1)}, bf16[18,4,768]{2,1,0:T(4,128)(2,1)S(1)}, u32[]{:S(2)}, u32[]{:S(2)}) collective-permute-start(bf16[18,4,768]{2,1,0:T(4,128)(2,1)S(1)} %get-tuple-element.16), channel_id=1, source_target_pairs={{15,0},{0,1},{1,2},{2,3},{3,4},{4,5},{5,6},{6,7},{7,8},{8,9},{9,10... | collective-permute-start | bytes 331784 | tf_op jit(solution)/shard_map/ppermute | solution.py:70
  87.1 2.1 %collective-permute-start.9 = (bf16[18,4,768]{2,1,0:T(4,128)(2,1)S(1)}, bf16[18,4,768]{2,1,0:T(4,128)(2,1)S(1)}, u32[]{:S(2)}, u32[]{:S(2)}) collective-permute-start(bf16[18,4,768]{2,1,0:T(4,128)(2,1)S(1)} %get-tuple-element.13), channel_id=1, source_target_pairs={{497,0},{498,1},{499,2},{500,3},{501,4},{502,5},{503,6},{504,7},{5... | collective-permute-start | bytes 331784 | tf_op jit(solution)/shard_map/ppermute | solution.py:70
  89.2 1.9 %collective-permute-start.10 = (bf16[18,4,768]{2,1,0:T(4,128)(2,1)S(1)}, bf16[18,4,768]{2,1,0:T(4,128)(2,1)S(1)}, u32[]{:S(2)}, u32[]{:S(2)}) collective-permute-start(bf16[18,4,768]{2,1,0:T(4,128)(2,1)S(1)} %get-tuple-element.14), channel_id=1, source_target_pairs={{496,0},{497,1},{498,2},{499,3},{500,4},{501,5},{502,6},{503,7},{5... | collective-permute-start | bytes 331784 | tf_op jit(solution)/shard_map/ppermute | solution.py:70
  91.1 0.7 collective-permute-done.11
  91.8 6.9 %collective-permute-done.9 = bf16[18,4,768]{2,1,0:T(4,128)(2,1)S(1)} collective-permute-done((bf16[18,4,768]{2,1,0:T(4,128)(2,1)S(1)}, bf16[18,4,768]{2,1,0:T(4,128)(2,1)S(1)}, u32[]{:S(2)}, u32[]{:S(2)}) %collective-permute-start.9) | collective-permute-done | bytes 110624 | tf_op jit(solution)/shard_map/ppermute | solution.py:70
  98.7 3.9 %collective-permute-done.10 = bf16[18,4,768]{2,1,0:T(4,128)(2,1)S(1)} collective-permute-done((bf16[18,4,768]{2,1,0:T(4,128)(2,1)S(1)}, bf16[18,4,768]{2,1,0:T(4,128)(2,1)S(1)}, u32[]{:S(2)}, u32[]{:S(2)}) %collective-permute-start.10) | collective-permute-done | bytes 110624 | tf_op jit(solution)/shard_map/ppermute | solution.py:70
  102.5 1.1 %maximum_bitcast_fusion = bf16[4,6,12,768]{3,0,2,1:T(4,128)(2,1)} fusion(bf16[3,6,4,768]{3,2,1,0:T(4,128)(2,1)S(1)} %bitcast.19, bf16[3,6,4,768]{3,2,1,0:T(4,128)(2,1)S(1)} %bitcast.21, bf16[3,6,4,768]{3,2,1,0:T(4,128)(2,1)S(1)} %bitcast.18, bf16[3,6,4,768]{3,2,1,0:T(4,128)(2,1)S(1)} %bitcast.20), kind=kLoop, calls=%fused_computation | loop fusion | flops 663552 | bytes 884736 | tf_op jit(solution)/shard_map/transpose | solution.py:367
  (10 shorter events, 0.1 us)
Async XLA Ops:
  14.9 44.3 %copy-start = (bf16[4,12,24,384]{3,2,1,0:T(8,128)(2,1)S(1)}, bf16[4,12,24,384]{3,2,1,0:T(8,128)(2,1)}, u32[]{:S(2)}) copy-start(bf16[4,12,24,384]{3,2,1,0:T(8,128)(2,1)} %param.8) | copy-start | bytes 2654212
  14.9 30.2 %collective-permute-start.2 = (bf16[4,288,384]{2,1,0:T(8,128)(2,1)S(1)}, bf16[4,288,384]{2,1,0:T(8,128)(2,1)S(1)}, u32[]{:S(2)}, u32[]{:S(2)}) collective-permute-start(bf16[4,288,384]{2,1,0:T(8,128)(2,1)S(1)} %all_to_all.5.a0), channel_id=1, source_target_pairs={{0,4},{1,5},{2,6},{3,7},{4,8},{5,9},{6,10},{7,11},{8,12},{9,13},{1... | collective-permute-start | bytes 2654216 | tf_op jit(solution)/shard_map/ppermute | solution.py:70
  19.7 35.1 %collective-permute-start.3 = (bf16[4,288,384]{2,1,0:T(8,128)(2,1)S(1)}, bf16[4,288,384]{2,1,0:T(8,128)(2,1)S(1)}, u32[]{:S(2)}, u32[]{:S(2)}) collective-permute-start(bf16[4,288,384]{2,1,0:T(8,128)(2,1)S(1)} %all_to_all.5.a0), channel_id=1, source_target_pairs={{0,268},{1,269},{2,270},{3,271},{4,0},{5,1},{6,2},{7,3},{8,4},{9,5... | collective-permute-start | bytes 2654216 | tf_op jit(solution)/shard_map/ppermute | solution.py:70
  21.7 35.1 %collective-permute-start.4 = (bf16[4,288,384]{2,1,0:T(8,128)(2,1)S(1)}, bf16[4,288,384]{2,1,0:T(8,128)(2,1)}, u32[]{:S(2)}, u32[]{:S(2)}) collective-permute-start(bf16[4,288,384]{2,1,0:T(8,128)(2,1)S(1)} %all_to_all.5.a0), channel_id=1, source_target_pairs={{0,8},{1,9},{2,10},{3,11},{4,268},{5,269},{6,270},{7,271},{8,256},... | collective-permute-start | bytes 2654216 | tf_op jit(solution)/shard_map/ppermute | solution.py:70
  26.1 33.1 %copy-start.1 = (f32[1536]{0:T(1024)S(1)}, f32[1536]{0:T(1024)}, u32[]{:S(2)}) copy-start(f32[1536]{0:T(1024)} %gain_hbm.1) | copy-start | bytes 18436
  26.1 33.1 %copy-start.2 = (f32[1536]{0:T(1024)S(1)}, f32[1536]{0:T(1024)}, u32[]{:S(2)}) copy-start(f32[1536]{0:T(1024)} %bias_hbm.1) | copy-start | bytes 18436
  28.5 47.4 %copy-start.3 = (f32[768]{0:T(1024)S(1)}, f32[768]{0:T(1024)}, u32[]{:S(2)}) copy-start(f32[768]{0:T(1024)} %gain_ref.1) | copy-start | bytes 9220
  28.5 47.4 %copy-start.4 = (f32[768]{0:T(1024)S(1)}, f32[768]{0:T(1024)}, u32[]{:S(2)}) copy-start(f32[768]{0:T(1024)} %bias_ref.1) | copy-start | bytes 9220
  28.5 30.7 %collective-permute-start = (bf16[576,384]{1,0:T(8,128)(2,1)}, bf16[576,384]{1,0:T(8,128)(2,1)S(1)}, u32[]{:S(2)}, u32[]{:S(2)}) collective-permute-start(bf16[576,384]{1,0:T(8,128)(2,1)} %left.1), channel_id=1, source_target_pairs={{0,496},{1,497},{2,498},{3,499},{4,500},{5,501},{6,502},{7,503},{8... | collective-permute-start | bytes 1327112 | tf_op jit(solution)/shard_map/ppermute | solution.py:70
  43.2 32.7 %collective-permute-start.5 = (bf16[4,288,384]{2,1,0:T(8,128)(2,1)S(1)}, bf16[4,288,384]{2,1,0:T(8,128)(2,1)S(1)}, u32[]{:S(2)}, u32[]{:S(2)}) collective-permute-start(bf16[4,288,384]{2,1,0:T(8,128)(2,1)S(1)} %all_to_all.5.a0), channel_id=1, source_target_pairs={{0,16},{1,17},{2,18},{3,19},{4,20},{5,21},{6,22},{7,23},{8,24},{9,... | collective-permute-start | bytes 2654216 | tf_op jit(solution)/shard_map/ppermute | solution.py:70
  45.1 30.8 %collective-permute-start.6 = (bf16[4,288,384]{2,1,0:T(8,128)(2,1)S(1)}, bf16[4,288,384]{2,1,0:T(8,128)(2,1)S(1)}, u32[]{:S(2)}, u32[]{:S(2)}) collective-permute-start(bf16[4,288,384]{2,1,0:T(8,128)(2,1)S(1)} %collective-permute-done.2.a1), channel_id=1, source_target_pairs={{0,16},{1,17},{2,18},{3,19},{4,20},{5,21},{6,22},{7,23},{8,24},{9,... | collective-permute-start | bytes 2654216 | tf_op jit(solution)/shard_map/ppermute | solution.py:70
  54.8 21.1 %collective-permute-start.7 = (bf16[4,288,384]{2,1,0:T(8,128)(2,1)S(1)}, bf16[4,288,384]{2,1,0:T(8,128)(2,1)S(1)}, u32[]{:S(2)}, u32[]{:S(2)}) collective-permute-start(bf16[4,288,384]{2,1,0:T(8,128)(2,1)S(1)} %collective-permute-done.3.a2), channel_id=1, source_target_pairs={{0,16},{1,17},{2,18},{3,19},{4,20},{5,21},{6,22},{7,23},{8,24},{9,... | collective-permute-start | bytes 2654216 | tf_op jit(solution)/shard_map/ppermute | solution.py:70
  56.8 19.1 %collective-permute-start.8 = (bf16[4,288,384]{2,1,0:T(8,128)(2,1)}, bf16[4,288,384]{2,1,0:T(8,128)(2,1)S(1)}, u32[]{:S(2)}, u32[]{:S(2)}) collective-permute-start(bf16[4,288,384]{2,1,0:T(8,128)(2,1)} %collective-permute-done.4.a3), channel_id=1, source_target_pairs={{0,16},{1,17},{2,18},{3,19},{4,20},{5,21},{6,22},{7,23},{8,24},{9,... | collective-permute-start | bytes 2654216 | tf_op jit(solution)/shard_map/ppermute | solution.py:70
  61.8 14.1 %collective-permute-start.1 = (bf16[144,1536]{1,0:T(8,128)(2,1)S(1)}, bf16[144,1536]{1,0:T(8,128)(2,1)S(1)}, u32[]{:S(2)}, u32[]{:S(2)}) collective-permute-start(bf16[144,1536]{1,0:T(8,128)(2,1)S(1)} %get-tuple-element.12), channel_id=1, source_target_pairs={{0,15},{1,0},{2,1},{3,2},{4,3},{5,4},{6,5},{7,6},{8,7},{9,8},{10,9... | collective-permute-start | bytes 1327112 | tf_op jit(solution)/shard_map/ppermute | solution.py:70
  85.1 6.6 %collective-permute-start.11 = (bf16[18,4,768]{2,1,0:T(4,128)(2,1)S(1)}, bf16[18,4,768]{2,1,0:T(4,128)(2,1)S(1)}, u32[]{:S(2)}, u32[]{:S(2)}) collective-permute-start(bf16[18,4,768]{2,1,0:T(4,128)(2,1)S(1)} %get-tuple-element.16), channel_id=1, source_target_pairs={{15,0},{0,1},{1,2},{2,3},{3,4},{4,5},{5,6},{6,7},{7,8},{8,9},{9,10... | collective-permute-start | bytes 331784 | tf_op jit(solution)/shard_map/ppermute | solution.py:70
  87.1 11.6 %collective-permute-start.9 = (bf16[18,4,768]{2,1,0:T(4,128)(2,1)S(1)}, bf16[18,4,768]{2,1,0:T(4,128)(2,1)S(1)}, u32[]{:S(2)}, u32[]{:S(2)}) collective-permute-start(bf16[18,4,768]{2,1,0:T(4,128)(2,1)S(1)} %get-tuple-element.13), channel_id=1, source_target_pairs={{497,0},{498,1},{499,2},{500,3},{501,4},{502,5},{503,6},{504,7},{5... | collective-permute-start | bytes 331784 | tf_op jit(solution)/shard_map/ppermute | solution.py:70
  89.2 13.3 %collective-permute-start.10 = (bf16[18,4,768]{2,1,0:T(4,128)(2,1)S(1)}, bf16[18,4,768]{2,1,0:T(4,128)(2,1)S(1)}, u32[]{:S(2)}, u32[]{:S(2)}) collective-permute-start(bf16[18,4,768]{2,1,0:T(4,128)(2,1)S(1)} %get-tuple-element.14), channel_id=1, source_target_pairs={{496,0},{497,1},{498,2},{499,3},{500,4},{501,5},{502,6},{503,7},{5... | collective-permute-start | bytes 331784 | tf_op jit(solution)/shard_map/ppermute | solution.py:70

commit v2 on v0

--- a/solution.py
+++ b/solution.py
@@ -84,14 +84,14 @@
     return centered * lax.rsqrt(spread + EPSILON) * gain + bias
 
 
-def cut_kernel(fine_ref, merge_hbm, qkv_hbm, out_hbm, left_ref, held_hbm, sems):
+def cut_kernel(fine_ref, merge_ref, qkv_ref, out_ref, left_ref, held_hbm, sems):
     core = lax.axis_index("lon") % 2
     for side in range(2):
 
         @pl.when(core == side)
         def _():
-            cuts = [(merge_hbm, side * 384, 0, 96), (out_hbm, side * 384, 240, 48)]
-            cuts += [(qkv_hbm, side * 1152 + n * 384, 96 + n * 48, 48) for n in range(3)]
+            cuts = [(merge_ref, side * 384, 0, 96), (out_ref, side * 384, 240, 48)]
+            cuts += [(qkv_ref, side * 1152 + n * 384, 96 + n * 48, 48) for n in range(3)]
             copies = []
             for member in range(4):
                 for n, (source, column, row, rows) in enumerate(cuts):
@@ -123,10 +123,12 @@
             jax.ShapeDtypeStruct((4, 288, 384), BF16),
         ),
         in_specs=[vmem] * 4,
-        out_specs=(vmem, vmem),
+        out_specs=(vmem, pl.BlockSpec(memory_space=pl.ANY)),
         scratch_shapes=[pltpu.SemaphoreType.DMA((20,))],
         name="cut",
-        cost_estimate=pl.CostEstimate(flops=1_000_000, bytes_accessed=1_800_000, transcendentals=0),
+        cost_estimate=pl.CostEstimate(
+            flops=200_000_000, bytes_accessed=3_000_000, transcendentals=0
+        ),
     )(fine, *weights)
 
 
@@ -187,6 +189,7 @@
         scratch_shapes=[pltpu.VMEM(value.shape, value.dtype) for value in operands]
         + [pltpu.SemaphoreType.DMA((4,))],
         name="patches",
+        compiler_params=pltpu.CompilerParams(vmem_limit_bytes=12 * 1024 * 1024),
         cost_estimate=pl.CostEstimate(
             flops=1_000_000_000, bytes_accessed=1_800_000, transcendentals=0
         ),
@@ -312,7 +315,7 @@
             pltpu.SemaphoreType.DMA((4,)),
         ],
         name="main",
-        compiler_params=pltpu.CompilerParams(vmem_limit_bytes=32 * 1024 * 1024),
+        compiler_params=pltpu.CompilerParams(vmem_limit_bytes=20 * 1024 * 1024),
         cost_estimate=pl.CostEstimate(
             flops=5_000_000_000, bytes_accessed=9_000_000, transcendentals=2_000_000
         ),

time: 110 us -> 107 us (0.973)
  local copies, waits for them, and re-layouts: 1.78 us -> 0.04 us
  Pallas kernels: 16.4 us -> 15 us
    unnamed x10 -> x12, local copies, waits for them, and re-layouts: 1.78 us -> 0.04 us
    pallas_call x1, Pallas kernels: 4.06 us -> 2.54 us  [patches(): pl.pallas_call(patch_kernel, out_shape=(pack, pack), in_specs=[pl.BlockSp...]
  transfers between devices with their start and end apart: 12 -> 12, of which waited for: 6 -> 6; matrix products, arithmetic and copies ran while one was open for 0% -> 0% of each run, Pallas kernels for 4% -> 2%
where the time goes in v2:
time: 107 us; the launch traced here: 106 us
  starting transfers between devices  40 us (37%)
  waiting for transfers between devices  37 us (35%)
  Pallas kernels  15 us (14%)
  blocking collectives  12.9 us (12%)
  other arithmetic  1.12 us (1%)
    ppermute x12, starting transfers between devices, moved(): return lax.ppermute(value, AXES, pairs)  40 us
    ppermute x12, waiting for transfers between devices, moved(): return lax.ppermute(value, AXES, pairs)  37 us
    all_to_all x1, blocking collectives, shards(): block = lax.all_to_all(held, AXES, 0, 0, axis_index_groups=near_groups())  12.9 us
    pallas_call x1, Pallas kernels, main(): pl.pallas_call(main_kernel, out_shape=(quad,) * 4, in_specs=[any_space] *...  9.26 us
    pallas_call x1, Pallas kernels, cut(): pl.pallas_call(cut_kernel, out_shape=(jax.ShapeDtypeStruct((576, 384), BF...  3.18 us
    pallas_call x1, Pallas kernels, patches(): pl.pallas_call(patch_kernel, out_shape=(pack, pack), in_specs=[pl.BlockSp...  2.54 us
  transfers between devices with their start and end apart: 12, of which 6 were waited for; matrix products, arithmetic and copies ran while one was open for 0% of the time, Pallas kernels for 2%

profile of v2, /device:TPU:62, one launch (start us, length us, event | category | flops | bytes accessed | tf_op | source)
XLA Modules:
  0.0 106.2 jit_solution(8606569374931250160)
XLA Ops:
  0.0 3.2 %cut.1 = (bf16[576,384]{1,0:T(8,128)(2,1)}, bf16[4,288,384]{2,1,0:T(8,128)(2,1)}) custom-call(bf16[1152,384]{1,0:T(8,128)(2,1)} %bitcast.15, bf16[96,768]{1,0:T(8,128)(2,1)} %merge_ref.1, bf16[48,2304]{1,0:T(8,128)(2,1)} %qkv_ref.1, bf16[48,768]{1,0:T(8,128)(2,1)} %out_ref.1), custom_call_target="tpu_custom_call" | custom-call | flops 200000000 | bytes 3000000 | tf_op jit(solution)/shard_map/cut/pallas_call | solution.py:119
  3.2 0.0 copy-start.5
  3.2 0.0 copy-start
  3.2 0.0 copy-start.1
  3.2 0.0 copy-start.2
  3.2 12.9 %all_to_all.5.a0 = bf16[4,288,384]{2,1,0:T(8,128)(2,1)S(1)} all-to-all(bf16[4,288,384]{2,1,0:T(8,128)(2,1)} %get-tuple-element.16), channel_id=1, replica_groups={{0,1,2,3},{4,5,6,7},{8,9,10,11},{12,13,14,15},{16,20,24,28},{17,21,25,2..., dimensions={0} | all-to-all | bytes 1769472 | tf_op jit(solution)/shard_map/all_to_all | solution.py:342
  16.1 6.2 %collective-permute-start.2 = (bf16[4,288,384]{2,1,0:T(8,128)(2,1)S(1)}, bf16[4,288,384]{2,1,0:T(8,128)(2,1)S(1)}, u32[]{:S(2)}, u32[]{:S(2)}) collective-permute-start(bf16[4,288,384]{2,1,0:T(8,128)(2,1)S(1)} %all_to_all.5.a0), channel_id=1, source_target_pairs={{0,4},{1,5},{2,6},{3,7},{4,8},{5,9},{6,10},{7,11},{8,12},{9,13},{1... | collective-permute-start | bytes 2654216 | tf_op jit(solution)/shard_map/ppermute | solution.py:70
  22.3 1.9 %collective-permute-start.3 = (bf16[4,288,384]{2,1,0:T(8,128)(2,1)S(1)}, bf16[4,288,384]{2,1,0:T(8,128)(2,1)S(1)}, u32[]{:S(2)}, u32[]{:S(2)}) collective-permute-start(bf16[4,288,384]{2,1,0:T(8,128)(2,1)S(1)} %all_to_all.5.a0), channel_id=1, source_target_pairs={{0,268},{1,269},{2,270},{3,271},{4,0},{5,1},{6,2},{7,3},{8,4},{9,5... | collective-permute-start | bytes 2654216 | tf_op jit(solution)/shard_map/ppermute | solution.py:70
  24.2 1.9 %collective-permute-start.4 = (bf16[4,288,384]{2,1,0:T(8,128)(2,1)S(1)}, bf16[4,288,384]{2,1,0:T(8,128)(2,1)S(1)}, u32[]{:S(2)}, u32[]{:S(2)}) collective-permute-start(bf16[4,288,384]{2,1,0:T(8,128)(2,1)S(1)} %all_to_all.5.a0), channel_id=1, source_target_pairs={{0,8},{1,9},{2,10},{3,11},{4,268},{5,269},{6,270},{7,271},{8,256},... | collective-permute-start | bytes 2654216 | tf_op jit(solution)/shard_map/ppermute | solution.py:70
  26.2 0.0 copy-start.3
  26.2 0.0 copy-start.4
  26.2 13.6 %collective-permute-start = (bf16[576,384]{1,0:T(8,128)(2,1)S(1)}, bf16[576,384]{1,0:T(8,128)(2,1)S(1)}, u32[]{:S(2)}, u32[]{:S(2)}) collective-permute-start(bf16[576,384]{1,0:T(8,128)(2,1)S(1)} %copy-done.5), channel_id=1, source_target_pairs={{0,496},{1,497},{2,498},{3,499},{4,500},{5,501},{6,502},{7,503},{8... | collective-permute-start | bytes 1327112 | tf_op jit(solution)/shard_map/ppermute | solution.py:70
  39.8 1.9 %collective-permute-start.5 = (bf16[4,288,384]{2,1,0:T(8,128)(2,1)S(1)}, bf16[4,288,384]{2,1,0:T(8,128)(2,1)S(1)}, u32[]{:S(2)}, u32[]{:S(2)}) collective-permute-start(bf16[4,288,384]{2,1,0:T(8,128)(2,1)S(1)} %all_to_all.5.a0), channel_id=1, source_target_pairs={{0,16},{1,17},{2,18},{3,19},{4,20},{5,21},{6,22},{7,23},{8,24},{9,... | collective-permute-start | bytes 2654216 | tf_op jit(solution)/shard_map/ppermute | solution.py:70
  41.8 9.8 %collective-permute-done.2.a1 = bf16[4,288,384]{2,1,0:T(8,128)(2,1)S(1)} collective-permute-done((bf16[4,288,384]{2,1,0:T(8,128)(2,1)S(1)}, bf16[4,288,384]{2,1,0:T(8,128)(2,1)S(1)}, u32[]{:S(2)}, u32[]{:S(2)}) %collective-permute-start.2) | collective-permute-done | bytes 884768 | tf_op jit(solution)/shard_map/ppermute | solution.py:70
  51.5 1.9 %collective-permute-start.6 = (bf16[4,288,384]{2,1,0:T(8,128)(2,1)S(1)}, bf16[4,288,384]{2,1,0:T(8,128)(2,1)S(1)}, u32[]{:S(2)}, u32[]{:S(2)}) collective-permute-start(bf16[4,288,384]{2,1,0:T(8,128)(2,1)S(1)} %collective-permute-done.2.a1), channel_id=1, source_target_pairs={{0,16},{1,17},{2,18},{3,19},{4,20},{5,21},{6,22},{7,23},{8,24},{9,... | collective-permute-start | bytes 2654216 | tf_op jit(solution)/shard_map/ppermute | solution.py:70
  53.5 3.9 %collective-permute-done.3.a2 = bf16[4,288,384]{2,1,0:T(8,128)(2,1)S(1)} collective-permute-done((bf16[4,288,384]{2,1,0:T(8,128)(2,1)S(1)}, bf16[4,288,384]{2,1,0:T(8,128)(2,1)S(1)}, u32[]{:S(2)}, u32[]{:S(2)}) %collective-permute-start.3) | collective-permute-done | bytes 884768 | tf_op jit(solution)/shard_map/ppermute | solution.py:70
  57.4 1.9 %collective-permute-start.7 = (bf16[4,288,384]{2,1,0:T(8,128)(2,1)S(1)}, bf16[4,288,384]{2,1,0:T(8,128)(2,1)S(1)}, u32[]{:S(2)}, u32[]{:S(2)}) collective-permute-start(bf16[4,288,384]{2,1,0:T(8,128)(2,1)S(1)} %collective-permute-done.3.a2), channel_id=1, source_target_pairs={{0,16},{1,17},{2,18},{3,19},{4,20},{5,21},{6,22},{7,23},{8,24},{9,... | collective-permute-start | bytes 2654216 | tf_op jit(solution)/shard_map/ppermute | solution.py:70
  59.3 0.0 collective-permute-done.4.a3
  59.3 2.4 %collective-permute-start.8 = (bf16[4,288,384]{2,1,0:T(8,128)(2,1)S(1)}, bf16[4,288,384]{2,1,0:T(8,128)(2,1)S(1)}, u32[]{:S(2)}, u32[]{:S(2)}) collective-permute-start(bf16[4,288,384]{2,1,0:T(8,128)(2,1)S(1)} %collective-permute-done.4.a3), channel_id=1, source_target_pairs={{0,16},{1,17},{2,18},{3,19},{4,20},{5,21},{6,22},{7,23},{8,24},{9,... | collective-permute-start | bytes 2654216 | tf_op jit(solution)/shard_map/ppermute | solution.py:70
  61.7 0.0 collective-permute-done.left_hbm
  61.8 2.5 %patches.1 = (bf16[144,1536]{1,0:T(8,128)(2,1)S(1)}, bf16[144,1536]{1,0:T(8,128)(2,1)S(1)}) custom-call(bf16[1152,384]{1,0:T(8,128)(2,1)S(1)} %bitcast.16, bf16[576,384]{1,0:T(8,128)(2,1)S(1)} %collective-permute-done.left_hbm, f32[1536]{0:T(1024)S(1)} %copy-done.1, f32[1536]{0:T(1024)S(1)} %copy-done.2), custom_call_target="tpu_custom_call" | custom-call | flops 1000000000 | bytes 1800000 | tf_op jit(solution)/shard_map/patches/pallas_call | solution.py:184
  64.3 2.2 %collective-permute-start.1 = (bf16[144,1536]{1,0:T(8,128)(2,1)S(1)}, bf16[144,1536]{1,0:T(8,128)(2,1)S(1)}, u32[]{:S(2)}, u32[]{:S(2)}) collective-permute-start(bf16[144,1536]{1,0:T(8,128)(2,1)S(1)} %get-tuple-element.15), channel_id=1, source_target_pairs={{0,15},{1,0},{2,1},{3,2},{4,3},{5,4},{6,5},{7,6},{8,7},{9,8},{10,9... | collective-permute-start | bytes 1327112 | tf_op jit(solution)/shard_map/ppermute | solution.py:70
  66.6 11.9 %collective-permute-done.1.p1 = bf16[144,1536]{1,0:T(8,128)(2,1)S(1)} collective-permute-done((bf16[144,1536]{1,0:T(8,128)(2,1)S(1)}, bf16[144,1536]{1,0:T(8,128)(2,1)S(1)}, u32[]{:S(2)}, u32[]{:S(2)}) %collective-permute-start.1) | collective-permute-done | bytes 442400 | tf_op jit(solution)/shard_map/ppermute | solution.py:70
  78.4 0.0 collective-permute-done.5.b0
  78.5 9.3 %main.1 = (bf16[18,4,768]{2,1,0:T(4,128)(2,1)S(1)}, bf16[18,4,768]{2,1,0:T(4,128)(2,1)S(1)}, bf16[18,4,768]{2,1,0:T(4,128)(2,1)S(1)}, bf16[18,4,768]{2,1,0:T(4,128)(2,1)S(1)}) custom-call(bf16[144,1536]{1,0:T(8,128)(2,1)S(1)} %get-tuple-element.14.p0, bf16[144,1536]{1,0:T(8,128)(2,1)S(1)} %collective-permute-done.1.p1, ...), custom_call_target="tpu_custom_call" | custom-call | flops 5000000000 | bytes 9000000 | tf_op jit(solution)/shard_map/main/pallas_call | solution.py:303
  87.7 1.9 %collective-permute-start.11 = (bf16[18,4,768]{2,1,0:T(4,128)(2,1)S(1)}, bf16[18,4,768]{2,1,0:T(4,128)(2,1)S(1)}, u32[]{:S(2)}, u32[]{:S(2)}) collective-permute-start(bf16[18,4,768]{2,1,0:T(4,128)(2,1)S(1)} %get-tuple-element.20), channel_id=1, source_target_pairs={{15,0},{0,1},{1,2},{2,3},{3,4},{4,5},{5,6},{6,7},{7,8},{8,9},{9,10... | collective-permute-start | bytes 331784 | tf_op jit(solution)/shard_map/ppermute | solution.py:70
  89.7 2.1 %collective-permute-start.9 = (bf16[18,4,768]{2,1,0:T(4,128)(2,1)S(1)}, bf16[18,4,768]{2,1,0:T(4,128)(2,1)S(1)}, u32[]{:S(2)}, u32[]{:S(2)}) collective-permute-start(bf16[18,4,768]{2,1,0:T(4,128)(2,1)S(1)} %get-tuple-element.17), channel_id=1, source_target_pairs={{497,0},{498,1},{499,2},{500,3},{501,4},{502,5},{503,6},{504,7},{5... | collective-permute-start | bytes 331784 | tf_op jit(solution)/shard_map/ppermute | solution.py:70
  91.8 1.9 %collective-permute-start.10 = (bf16[18,4,768]{2,1,0:T(4,128)(2,1)S(1)}, bf16[18,4,768]{2,1,0:T(4,128)(2,1)S(1)}, u32[]{:S(2)}, u32[]{:S(2)}) collective-permute-start(bf16[18,4,768]{2,1,0:T(4,128)(2,1)S(1)} %get-tuple-element.18), channel_id=1, source_target_pairs={{496,0},{497,1},{498,2},{499,3},{500,4},{501,5},{502,6},{503,7},{5... | collective-permute-start | bytes 331784 | tf_op jit(solution)/shard_map/ppermute | solution.py:70
  93.7 0.7 collective-permute-done.11
  94.4 6.8 %collective-permute-done.9 = bf16[18,4,768]{2,1,0:T(4,128)(2,1)S(1)} collective-permute-done((bf16[18,4,768]{2,1,0:T(4,128)(2,1)S(1)}, bf16[18,4,768]{2,1,0:T(4,128)(2,1)S(1)}, u32[]{:S(2)}, u32[]{:S(2)}) %collective-permute-start.9) | collective-permute-done | bytes 110624 | tf_op jit(solution)/shard_map/ppermute | solution.py:70
  101.2 4.0 %collective-permute-done.10 = bf16[18,4,768]{2,1,0:T(4,128)(2,1)S(1)} collective-permute-done((bf16[18,4,768]{2,1,0:T(4,128)(2,1)S(1)}, bf16[18,4,768]{2,1,0:T(4,128)(2,1)S(1)}, u32[]{:S(2)}, u32[]{:S(2)}) %collective-permute-start.10) | collective-permute-done | bytes 110624 | tf_op jit(solution)/shard_map/ppermute | solution.py:70
  105.2 1.1 %maximum_bitcast_fusion = bf16[4,6,12,768]{3,0,2,1:T(4,128)(2,1)} fusion(bf16[3,6,4,768]{3,2,1,0:T(4,128)(2,1)S(1)} %bitcast.19, bf16[3,6,4,768]{3,2,1,0:T(4,128)(2,1)S(1)} %bitcast.21, bf16[3,6,4,768]{3,2,1,0:T(4,128)(2,1)S(1)} %bitcast.18, bf16[3,6,4,768]{3,2,1,0:T(4,128)(2,1)S(1)} %bitcast.20), kind=kLoop, calls=%fused_computation | loop fusion | flops 663552 | bytes 884736 | tf_op jit(solution)/shard_map/transpose | solution.py:359
  (11 shorter events, 0.1 us)
Async XLA Ops:
  3.2 23.0 %copy-start.5 = (bf16[576,384]{1,0:T(8,128)(2,1)S(1)}, bf16[576,384]{1,0:T(8,128)(2,1)}, u32[]{:S(2)}) copy-start(bf16[576,384]{1,0:T(8,128)(2,1)} %get-tuple-element.13) | copy-start | bytes 1327108
  3.2 58.6 %copy-start = (bf16[4,12,24,384]{3,2,1,0:T(8,128)(2,1)S(1)}, bf16[4,12,24,384]{3,2,1,0:T(8,128)(2,1)}, u32[]{:S(2)}) copy-start(bf16[4,12,24,384]{3,2,1,0:T(8,128)(2,1)} %param.8) | copy-start | bytes 2654212
  3.2 58.5 %copy-start.1 = (f32[1536]{0:T(1024)S(1)}, f32[1536]{0:T(1024)}, u32[]{:S(2)}) copy-start(f32[1536]{0:T(1024)} %gain_hbm.1) | copy-start | bytes 18436
  3.2 58.5 %copy-start.2 = (f32[1536]{0:T(1024)S(1)}, f32[1536]{0:T(1024)}, u32[]{:S(2)}) copy-start(f32[1536]{0:T(1024)} %bias_hbm.1) | copy-start | bytes 18436
  16.1 35.4 %collective-permute-start.2 = (bf16[4,288,384]{2,1,0:T(8,128)(2,1)S(1)}, bf16[4,288,384]{2,1,0:T(8,128)(2,1)S(1)}, u32[]{:S(2)}, u32[]{:S(2)}) collective-permute-start(bf16[4,288,384]{2,1,0:T(8,128)(2,1)S(1)} %all_to_all.5.a0), channel_id=1, source_target_pairs={{0,4},{1,5},{2,6},{3,7},{4,8},{5,9},{6,10},{7,11},{8,12},{9,13},{1... | collective-permute-start | bytes 2654216 | tf_op jit(solution)/shard_map/ppermute | solution.py:70
  22.3 35.1 %collective-permute-start.3 = (bf16[4,288,384]{2,1,0:T(8,128)(2,1)S(1)}, bf16[4,288,384]{2,1,0:T(8,128)(2,1)S(1)}, u32[]{:S(2)}, u32[]{:S(2)}) collective-permute-start(bf16[4,288,384]{2,1,0:T(8,128)(2,1)S(1)} %all_to_all.5.a0), channel_id=1, source_target_pairs={{0,268},{1,269},{2,270},{3,271},{4,0},{5,1},{6,2},{7,3},{8,4},{9,5... | collective-permute-start | bytes 2654216 | tf_op jit(solution)/shard_map/ppermute | solution.py:70
  24.2 35.1 %collective-permute-start.4 = (bf16[4,288,384]{2,1,0:T(8,128)(2,1)S(1)}, bf16[4,288,384]{2,1,0:T(8,128)(2,1)S(1)}, u32[]{:S(2)}, u32[]{:S(2)}) collective-permute-start(bf16[4,288,384]{2,1,0:T(8,128)(2,1)S(1)} %all_to_all.5.a0), channel_id=1, source_target_pairs={{0,8},{1,9},{2,10},{3,11},{4,268},{5,269},{6,270},{7,271},{8,256},... | collective-permute-start | bytes 2654216 | tf_op jit(solution)/shard_map/ppermute | solution.py:70
  26.2 52.3 %copy-start.3 = (f32[768]{0:T(1024)S(1)}, f32[768]{0:T(1024)}, u32[]{:S(2)}) copy-start(f32[768]{0:T(1024)} %gain_ref.1) | copy-start | bytes 9220
  26.2 52.3 %copy-start.4 = (f32[768]{0:T(1024)S(1)}, f32[768]{0:T(1024)}, u32[]{:S(2)}) copy-start(f32[768]{0:T(1024)} %bias_ref.1) | copy-start | bytes 9220
  26.2 35.6 %collective-permute-start = (bf16[576,384]{1,0:T(8,128)(2,1)S(1)}, bf16[576,384]{1,0:T(8,128)(2,1)S(1)}, u32[]{:S(2)}, u32[]{:S(2)}) collective-permute-start(bf16[576,384]{1,0:T(8,128)(2,1)S(1)} %copy-done.5), channel_id=1, source_target_pairs={{0,496},{1,497},{2,498},{3,499},{4,500},{5,501},{6,502},{7,503},{8... | collective-permute-start | bytes 1327112 | tf_op jit(solution)/shard_map/ppermute | solution.py:70
  39.8 38.6 %collective-permute-start.5 = (bf16[4,288,384]{2,1,0:T(8,128)(2,1)S(1)}, bf16[4,288,384]{2,1,0:T(8,128)(2,1)S(1)}, u32[]{:S(2)}, u32[]{:S(2)}) collective-permute-start(bf16[4,288,384]{2,1,0:T(8,128)(2,1)S(1)} %all_to_all.5.a0), channel_id=1, source_target_pairs={{0,16},{1,17},{2,18},{3,19},{4,20},{5,21},{6,22},{7,23},{8,24},{9,... | collective-permute-start | bytes 2654216 | tf_op jit(solution)/shard_map/ppermute | solution.py:70
  51.5 26.9 %collective-permute-start.6 = (bf16[4,288,384]{2,1,0:T(8,128)(2,1)S(1)}, bf16[4,288,384]{2,1,0:T(8,128)(2,1)S(1)}, u32[]{:S(2)}, u32[]{:S(2)}) collective-permute-start(bf16[4,288,384]{2,1,0:T(8,128)(2,1)S(1)} %collective-permute-done.2.a1), channel_id=1, source_target_pairs={{0,16},{1,17},{2,18},{3,19},{4,20},{5,21},{6,22},{7,23},{8,24},{9,... | collective-permute-start | bytes 2654216 | tf_op jit(solution)/shard_map/ppermute | solution.py:70
  57.4 21.0 %collective-permute-start.7 = (bf16[4,288,384]{2,1,0:T(8,128)(2,1)S(1)}, bf16[4,288,384]{2,1,0:T(8,128)(2,1)S(1)}, u32[]{:S(2)}, u32[]{:S(2)}) collective-permute-start(bf16[4,288,384]{2,1,0:T(8,128)(2,1)S(1)} %collective-permute-done.3.a2), channel_id=1, source_target_pairs={{0,16},{1,17},{2,18},{3,19},{4,20},{5,21},{6,22},{7,23},{8,24},{9,... | collective-permute-start | bytes 2654216 | tf_op jit(solution)/shard_map/ppermute | solution.py:70
  59.3 19.1 %collective-permute-start.8 = (bf16[4,288,384]{2,1,0:T(8,128)(2,1)S(1)}, bf16[4,288,384]{2,1,0:T(8,128)(2,1)S(1)}, u32[]{:S(2)}, u32[]{:S(2)}) collective-permute-start(bf16[4,288,384]{2,1,0:T(8,128)(2,1)S(1)} %collective-permute-done.4.a3), channel_id=1, source_target_pairs={{0,16},{1,17},{2,18},{3,19},{4,20},{5,21},{6,22},{7,23},{8,24},{9,... | collective-permute-start | bytes 2654216 | tf_op jit(solution)/shard_map/ppermute | solution.py:70
  64.3 14.1 %collective-permute-start.1 = (bf16[144,1536]{1,0:T(8,128)(2,1)S(1)}, bf16[144,1536]{1,0:T(8,128)(2,1)S(1)}, u32[]{:S(2)}, u32[]{:S(2)}) collective-permute-start(bf16[144,1536]{1,0:T(8,128)(2,1)S(1)} %get-tuple-element.15), channel_id=1, source_target_pairs={{0,15},{1,0},{2,1},{3,2},{4,3},{5,4},{6,5},{7,6},{8,7},{9,8},{10,9... | collective-permute-start | bytes 1327112 | tf_op jit(solution)/shard_map/ppermute | solution.py:70
  87.7 6.6 %collective-permute-start.11 = (bf16[18,4,768]{2,1,0:T(4,128)(2,1)S(1)}, bf16[18,4,768]{2,1,0:T(4,128)(2,1)S(1)}, u32[]{:S(2)}, u32[]{:S(2)}) collective-permute-start(bf16[18,4,768]{2,1,0:T(4,128)(2,1)S(1)} %get-tuple-element.20), channel_id=1, source_target_pairs={{15,0},{0,1},{1,2},{2,3},{3,4},{4,5},{5,6},{6,7},{7,8},{8,9},{9,10... | collective-permute-start | bytes 331784 | tf_op jit(solution)/shard_map/ppermute | solution.py:70
  89.7 11.5 %collective-permute-start.9 = (bf16[18,4,768]{2,1,0:T(4,128)(2,1)S(1)}, bf16[18,4,768]{2,1,0:T(4,128)(2,1)S(1)}, u32[]{:S(2)}, u32[]{:S(2)}) collective-permute-start(bf16[18,4,768]{2,1,0:T(4,128)(2,1)S(1)} %get-tuple-element.17), channel_id=1, source_target_pairs={{497,0},{498,1},{499,2},{500,3},{501,4},{502,5},{503,6},{504,7},{5... | collective-permute-start | bytes 331784 | tf_op jit(solution)/shard_map/ppermute | solution.py:70
  91.8 13.4 %collective-permute-start.10 = (bf16[18,4,768]{2,1,0:T(4,128)(2,1)S(1)}, bf16[18,4,768]{2,1,0:T(4,128)(2,1)S(1)}, u32[]{:S(2)}, u32[]{:S(2)}) collective-permute-start(bf16[18,4,768]{2,1,0:T(4,128)(2,1)S(1)} %get-tuple-element.18), channel_id=1, source_target_pairs={{496,0},{497,1},{498,2},{499,3},{500,4},{501,5},{502,6},{503,7},{5... | collective-permute-start | bytes 331784 | tf_op jit(solution)/shard_map/ppermute | solution.py:70
